TPU v7x, 128 devices: a whole 4x4x4 slice. The times are simulated.
128 devices in a mesh: dp: 32 (over x, y, z_lo), seq: 4 (over z_hi, core).
Axes of the slice: x: 4, y: 4, z: 4 (z_hi: 2, z_lo: 2; z = z_hi * 2 + z_lo), core: 2. Of those that a mesh axis runs over, the one named last changes fastest.
Arguments:
- qkv: bfloat16 [64, 1024, 4608], P('dp', 'seq'), may hold values from -20.4 to 20.4
- gate: float32 [64, 3072], P('dp'), may hold values from 0.5 to 2.5
- cotangent: bfloat16 [64, 1024, 3072], P('dp', 'seq'), may hold values from -6 to 6
- out_weight: bfloat16 [1536, 3072], replicated, may hold values from -0.15625 to 0.15625
- clip_lengths: int32 [64], replicated, may hold values from 1 to 768, as said below
- text_lengths: int32 [64], replicated, may hold values from 1 to 256, as said below
- plan: int32 [32], replicated, may hold values from 0 to 31, as said below
Outputs:
- mixed: bfloat16 [64, 1024, 3072], P('dp', 'seq')
- gate_grad: float32 [64, 3072], P('dp')
- weight_grad: float32 [1536, 3072], P(None, ('dp', 'seq'))
- qkv_grad: bfloat16 [64, 1024, 4608], P('dp', 'seq')
Inputs may be any that keep to these rules, and one draw needn't show every extreme that they name: clip_lengths[c] counts the live video positions of source clip c = 2 g + s (group g, slot s); some clip has exactly 768. text_lengths[c] counts the live text positions of source clip c; some clip has exactly 256. plan is a permutation of 0 to 31: the second clip of group g becomes the second clip of group plan[g].
All inputs are finite; a program needn't handle non-finite values.
Results may differ from a plain program's by a relative error of at most 0.011.
Values may be sent and summed in bfloat16 or wider, within the bound.
No kernel may reach another device: no remote copies, remote signals or barrier semaphores. Data moves between devices by JAX's collectives and lax.ppermute only.
A program may use at most 128 MiB of HBM per device.

v0:
```python
import jax
import jax.numpy as jnp
from jax import lax
from jax.sharding import PartitionSpec as P

HD = 128
TXT = 256
BLOCK = 512
NEGATIVE = -1e30


def from_everyone(x, axis):
    copies = jnp.broadcast_to(x, (lax.axis_size(axis), *x.shape))
    return lax.all_to_all(copies, axis, split_axis=0, concat_axis=0, tiled=True)


def taken_together(x, axis):
    everything = from_everyone(x, axis)
    return jnp.sum(everything, axis=0)


def allowed_rows(offset, count, text_len, video_len):
    places = offset + jnp.arange(count, dtype=jnp.int32)
    return (places < text_len) | (places >= TXT) & (places < TXT + video_len)


def move_in(block_rows, inverse):
    groups = lax.axis_size("dp")
    portions = block_rows.reshape(groups, block_rows.shape[0] // groups, block_rows.shape[1])
    spread = lax.all_to_all(portions, "dp", split_axis=0, concat_axis=0, tiled=True)
    arranged = jnp.take(spread, inverse, axis=0)
    landed = lax.all_to_all(arranged, "dp", split_axis=0, concat_axis=0, tiled=True)
    return landed.reshape(block_rows.shape)


def move_out(block_rows, plan):
    groups = lax.axis_size("dp")
    portions = block_rows.reshape(groups, block_rows.shape[0] // groups, block_rows.shape[1])
    spread = lax.all_to_all(portions, "dp", split_axis=0, concat_axis=0, tiled=True)
    arranged = jnp.take(spread, plan, axis=0)
    landed = lax.all_to_all(arranged, "dp", split_axis=0, concat_axis=0, tiled=True)
    return landed.reshape(block_rows.shape)


def to_heads(tokens, seq_ways):
    clip_count, row_count, full_width = tokens.shape
    local_width = full_width // (3 * seq_ways)
    parted = tokens.reshape(clip_count, row_count, 3, seq_ways, local_width)
    exchanged = lax.all_to_all(parted, "seq", split_axis=3, concat_axis=1, tiled=True)
    return exchanged.reshape(clip_count, row_count * seq_ways, 3, local_width)


def block_scores(query_rows, key_rows, query_ok, key_ok, score_scale):
    scores = (
        jnp.einsum("qhd,khd->hqk", query_rows, key_rows, preferred_element_type=jnp.float32)
        * score_scale
    )
    live_pairs = query_ok[None, :, None] & key_ok[None, None, :]
    return (scores, live_pairs)


def attend(queries, keys_all, values_all, text_len, video_len, score_scale):
    seq_len, head_count, head_dim = queries.shape
    block_count = (TXT + video_len + BLOCK - 1) // BLOCK

    def query_step(query_block, built):
        results, log_totals = built
        offset = query_block * BLOCK
        query_rows = lax.dynamic_slice_in_dim(queries, offset, BLOCK, 0)
        query_ok = allowed_rows(offset, BLOCK, text_len, video_len)

        def scored(key_block):
            key_offset = key_block * BLOCK
            key_rows = lax.dynamic_slice_in_dim(keys_all, key_offset, BLOCK, 0)
            key_ok = allowed_rows(key_offset, BLOCK, text_len, video_len)
            scores, live_pairs = block_scores(query_rows, key_rows, query_ok, key_ok, score_scale)
            return (scores, live_pairs, key_offset)

        def stats_step(key_block, running):
            row_peak, row_total = running
            scores, live_pairs, key_offset = scored(key_block)
            masked = jnp.where(live_pairs, scores, NEGATIVE)
            new_peak = jnp.maximum(row_peak, jnp.max(masked, axis=-1))
            row_total = row_total * jnp.exp(row_peak - new_peak) + jnp.sum(
                jnp.exp(masked - new_peak[..., None]), axis=-1
            )
            return (new_peak, row_total)

        start_peak = jnp.full((head_count, BLOCK), NEGATIVE, jnp.float32)
        row_peak, row_total = lax.fori_loop(
            0, block_count, stats_step, (start_peak, jnp.zeros((head_count, BLOCK), jnp.float32))
        )
        log_total = row_peak + jnp.log(row_total)

        def value_step(key_block, partial_sums):
            scores, live_pairs, key_offset = scored(key_block)
            probs_low = jnp.exp(
                jnp.where(live_pairs, scores - log_total[..., None], NEGATIVE)
            ).astype(jnp.bfloat16)
            value_rows = lax.dynamic_slice_in_dim(values_all, key_offset, BLOCK, 0)
            return partial_sums + jnp.einsum(
                "hqk,khd->qhd", probs_low, value_rows, preferred_element_type=jnp.float32
            )

        partial_sums = lax.fori_loop(
            0, block_count, value_step, jnp.zeros((BLOCK, head_count, head_dim), jnp.float32)
        )
        results = lax.dynamic_update_slice_in_dim(
            results, partial_sums.astype(jnp.bfloat16), offset, 0
        )
        log_totals = lax.dynamic_update_slice_in_dim(log_totals, log_total, offset, 1)
        return (results, log_totals)

    initial = (
        jnp.zeros((seq_len, head_count, head_dim), jnp.bfloat16),
        jnp.zeros((head_count, seq_len), jnp.float32),
    )
    return lax.fori_loop(0, block_count, query_step, initial)


def attend_back(
    queries, keys_all, values_all, results, d_results, log_totals, text_len, video_len, score_scale
):
    seq_len, head_count, head_dim = queries.shape
    block_count = (TXT + video_len + BLOCK - 1) // BLOCK
    row_dots_all = jnp.einsum("qhd,qhd->hq", d_results, results, preferred_element_type=jnp.float32)

    def query_step(query_block, gradients):
        grad_q, grad_k, grad_v = gradients
        offset = query_block * BLOCK
        query_rows = lax.dynamic_slice_in_dim(queries, offset, BLOCK, 0)
        d_rows = lax.dynamic_slice_in_dim(d_results, offset, BLOCK, 0)
        query_ok = allowed_rows(offset, BLOCK, text_len, video_len)
        log_total = lax.dynamic_slice_in_dim(log_totals, offset, BLOCK, 1)
        row_dots = lax.dynamic_slice_in_dim(row_dots_all, offset, BLOCK, 1)

        def key_step(key_block, inner_state):
            q_sums, grad_k, grad_v = inner_state
            key_offset = key_block * BLOCK
            key_rows = lax.dynamic_slice_in_dim(keys_all, key_offset, BLOCK, 0)
            value_rows = lax.dynamic_slice_in_dim(values_all, key_offset, BLOCK, 0)
            key_ok = allowed_rows(key_offset, BLOCK, text_len, video_len)
            scores, live_pairs = block_scores(query_rows, key_rows, query_ok, key_ok, score_scale)
            probabilities = jnp.exp(jnp.where(live_pairs, scores - log_total[..., None], NEGATIVE))
            probs_low = probabilities.astype(jnp.bfloat16)
            d_probs = jnp.einsum(
                "qhd,khd->hqk", d_rows, value_rows, preferred_element_type=jnp.float32
            )
            d_scores = (probabilities * (d_probs - row_dots[..., None])).astype(jnp.bfloat16)
            q_sums = q_sums + jnp.einsum(
                "hqk,khd->qhd", d_scores, key_rows, preferred_element_type=jnp.float32
            )
            k_part = jnp.einsum(
                "hqk,qhd->khd", d_scores, query_rows, preferred_element_type=jnp.float32
            )
            v_part = jnp.einsum(
                "hqk,qhd->khd", probs_low, d_rows, preferred_element_type=jnp.float32
            )
            grad_k = lax.dynamic_update_slice_in_dim(
                grad_k,
                lax.dynamic_slice_in_dim(grad_k, key_offset, BLOCK, 0) + k_part,
                key_offset,
                0,
            )
            grad_v = lax.dynamic_update_slice_in_dim(
                grad_v,
                lax.dynamic_slice_in_dim(grad_v, key_offset, BLOCK, 0) + v_part,
                key_offset,
                0,
            )
            return (q_sums, grad_k, grad_v)

        q_start = jnp.zeros((BLOCK, head_count, head_dim), jnp.float32)
        q_sums, grad_k, grad_v = lax.fori_loop(0, block_count, key_step, (q_start, grad_k, grad_v))
        grad_q = lax.dynamic_update_slice_in_dim(grad_q, q_sums, offset, 0)
        return (grad_q, grad_k, grad_v)

    zero_grad = jnp.zeros((seq_len, head_count, head_dim), jnp.float32)
    grad_q, grad_k, grad_v = lax.fori_loop(
        0, block_count, query_step, (zero_grad, zero_grad, zero_grad)
    )
    return (
        (grad_q * score_scale).astype(jnp.bfloat16),
        (grad_k * score_scale).astype(jnp.bfloat16),
        grad_v.astype(jnp.bfloat16),
    )


def body(qkv, gate, cotangent, out_weight, clip_lengths, text_lengths, plan):
    groups = lax.axis_size("dp")
    seq_ways = lax.axis_size("seq")
    group_index = lax.axis_index("dp")
    seq_index = lax.axis_index("seq")
    ordinal = jnp.arange(groups, dtype=jnp.int32)
    inverse = jnp.sum(jnp.where(plan[None, :] == ordinal[:, None], ordinal[None, :], 0), axis=1)
    home_clip = 2 * group_index
    head_width = out_weight.shape[0]
    local_width = head_width // seq_ways
    head_count = local_width // HD
    row_count = cotangent.shape[1]
    score_scale = HD ** (-0.5)
    arrived = move_in(qkv[1], inverse)
    working = jnp.stack([qkv[0], arrived])
    clip_ids = (home_clip, 2 * inverse[group_index] + 1)
    spread_heads = to_heads(working, seq_ways)
    seq_len = spread_heads.shape[1]
    video_lens = [clip_lengths[clip_id] for clip_id in clip_ids]
    text_lens = [text_lengths[clip_id] for clip_id in clip_ids]
    sections = []
    result_list = []
    log_list = []
    for slot_index in range(2):
        triple = [
            spread_heads[slot_index, :, member].reshape(seq_len, head_count, HD)
            for member in range(3)
        ]
        results, log_totals = attend(
            triple[0],
            triple[1],
            triple[2],
            text_lens[slot_index],
            video_lens[slot_index],
            score_scale,
        )
        sections.append(triple)
        result_list.append(results)
        log_list.append(log_totals)
    attn_heads = jnp.stack(result_list).reshape(2, seq_len, 1, local_width)
    attn_back = lax.all_to_all(attn_heads, "seq", split_axis=1, concat_axis=2, tiled=True).reshape(
        2, row_count, head_width
    )
    outputs = jnp.einsum("crh,hd->crd", attn_back, out_weight, preferred_element_type=jnp.float32)
    mixed = (gate[:, None, :] * outputs).astype(jnp.bfloat16)
    gate_grad = taken_together(jnp.sum(cotangent.astype(jnp.float32) * outputs, axis=1), "seq")
    scaled = (cotangent.astype(jnp.float32) * gate[:, None, :]).astype(jnp.bfloat16)
    weight_rows = lax.dynamic_slice_in_dim(out_weight, seq_index * local_width, local_width, 0)
    flat_heads = attn_heads.reshape(2, seq_len, local_width)
    portion = lax.all_gather(scaled, "seq", axis=1, tiled=True)
    weight_part = jnp.einsum("cnh,cnd->hd", flat_heads, portion, preferred_element_type=jnp.float32)
    grad_rows = jnp.einsum(
        "cnd,hd->cnh", portion, weight_rows, preferred_element_type=jnp.float32
    ).astype(jnp.bfloat16)
    d_heads, weight_part = (grad_rows, weight_part)
    summed = lax.psum_scatter(weight_part, "dp", scatter_dimension=1, tiled=True)
    weight_grad = lax.all_to_all(summed, "seq", split_axis=1, concat_axis=0, tiled=True)
    grad_list = []
    for slot_index in range(2):
        triple = sections[slot_index]
        d_rows = d_heads[slot_index].reshape(seq_len, head_count, HD)
        grad_parts = attend_back(
            triple[0],
            triple[1],
            triple[2],
            result_list[slot_index],
            d_rows,
            log_list[slot_index],
            text_lens[slot_index],
            video_lens[slot_index],
            score_scale,
        )
        grad_list.append(
            jnp.stack([grad_part.reshape(seq_len, local_width) for grad_part in grad_parts], axis=1)
        )
    grad_heads = jnp.stack(grad_list).reshape(2, seq_len, 3, 1, local_width)
    grad_tokens = lax.all_to_all(
        grad_heads, "seq", split_axis=1, concat_axis=3, tiled=True
    ).reshape(2, row_count, 3 * head_width)
    grad_tokens = jnp.stack([grad_tokens[0], move_out(grad_tokens[1], plan)])
    return (mixed, gate_grad, weight_grad, grad_tokens)


def solution(mesh):
    in_specs = (P("dp", "seq", None), P("dp", None), P("dp", "seq", None), P(), P(), P(), P())
    out_specs = (P("dp", "seq", None), P("dp", None), P(None, ("dp", "seq")), P("dp", "seq", None))
    return jax.shard_map(body, mesh=mesh, in_specs=in_specs, out_specs=out_specs, check_vma=False)
```

profile of v0, /device:TPU:1, one launch (start us, length us, event | category | flops | bytes accessed | tf_op | source)
XLA Modules:
  0.0 709.6 jit_solution(8524687649885798854)
XLA Ops:
  7.2 4.9 fusion.183
  12.0 9.3 %all-to-all-start = ((bf16[32,8,4608]{2,1,0:T(8,128)(2,1)}), bf16[32,8,4608]{2,1,0:T(8,128)(2,1)S(1)}, u32[]{:S(2)}, u32[]{:S(2)}) async-start(bf16[32,8,4608]{2,1,0:T(8,128)(2,1)} %get-tuple-element.2898), calls=%async_computation | async-start | bytes 4718592 | tf_op jit(solution)/shard_map/all_to_all | solution.py:30
  21.5 30.6 %all-to-all-done = bf16[32,8,4608]{2,1,0:T(8,128)(2,1)S(1)} async-done(((bf16[32,8,4608]{2,1,0:T(8,128)(2,1)}), bf16[32,8,4608]{2,1,0:T(8,128)(2,1)S(1)}, u32[]{:S(2)}, u32[]{:S(2)}) %all-to-all-start) | async-done | bytes 2359328 | tf_op jit(solution)/shard_map/all_to_all | solution.py:30
  54.3 3.3 broadcast_select_fusion.1
  57.6 4.2 all-to-all-start.1
  61.9 4.3 copy.392
  66.1 25.9 %all-to-all-done.1 = bf16[32,8,4608]{2,1,0:T(8,128)(2,1)S(1)} async-done(((bf16[32,8,4608]{2,1,0:T(8,128)(2,1)}), bf16[32,8,4608]{2,1,0:T(8,128)(2,1)S(1)}, u32[]{:S(2)}, u32[]{:S(2)}) %all-to-all-start.1) | async-done | bytes 2359328 | tf_op jit(solution)/shard_map/all_to_all | solution.py:32
  94.1 5.5 copy.325
  101.8 2.5 copy.326
  104.3 8.3 %all-to-all-start.2 = ((bf16[2,256,3,4,384]{1,4,2,0,3:T(8,128)(2,1)}), bf16[2,256,3,4,384]{1,4,2,0,3:T(8,128)(2,1)}, u32[]{:S(2)}, u32[]{:S(2)}) async-start(bf16[2,256,3,4,384]{1,4,2,0,3:T(8,128)(2,1)} %copy.326), calls=%async_computation.2 | async-start | bytes 9437184 | tf_op jit(solution)/shard_map/all_to_all | solution.py:49
  117.0 49.8 %all-to-all-done.2 = bf16[2,256,3,4,384]{1,4,2,0,3:T(8,128)(2,1)} async-done(((bf16[2,256,3,4,384]{1,4,2,0,3:T(8,128)(2,1)}), bf16[2,256,3,4,384]{1,4,2,0,3:T(8,128)(2,1)}, u32[]{:S(2)}, u32[]{:S(2)}) %all-to-all-start.2) | async-done | bytes 4718624 | tf_op jit(solution)/shard_map/all_to_all | solution.py:49
  166.9 6.6 copy.327
  173.5 4.0 fusion.182
  181.5 25.5 %while.235 = (s32[]{:T(128)}, bf16[1024,3,128]{0,2,1:T(8,128)(2,1)S(1)}, f32[3,1024]{1,0:T(4,128)}, s32[]{:T(128)}, bf16[1024,3,128]{2,0,1:T(8,128)(2,1)}, /*ind...) while((s32[]{:T(128)}, ...), condition=%wide.region_16.18_spmd, body=%wide.region_9.17_spmd.sunk | while | flops 613564928 | bytes 14026645 | solution.py:118
  182.5 4.5 while.242
  187.8 6.3 while.243
  188.6 2.4 fusion.293
  191.7 2.4 fusion.293
  195.3 4.5 while.242
  200.5 6.3 while.243
  201.3 2.4 fusion.293
  204.5 2.4 fusion.293
  207.0 2.6 copy.328
  209.6 2.3 copy.331
  214.6 2.3 copy.330
  218.5 8.6 %while.232 = (s32[]{:T(128)}, bf16[1024,3,128]{0,2,1:T(8,128)(2,1)}, f32[3,1024]{1,0:T(4,128)}, s32[]{:T(128)}, bf16[1024,3,128]{2,0,1:T(8,128)(2,1)}, /*index=5...) while((s32[]{:T(128)}, bf16[1024,3,128]{0,2,1:T(8,128)(2,1)}, ...), condition=%wide.region_8.10_spmd, body=%wide.region_1.9_spmd.sunk | while | flops 613564928 | bytes 14026645 | solution.py:118
  220.0 2.3 while.240
  223.0 3.2 while.241
  223.9 2.4 fusion.301
  227.1 2.9 pad_maximum_fusion.2
  230.0 4.3 copy.338
  234.3 24.0 %all_to_all.89 = bf16[2,1024,1,384]{3,0,2,1:T(2,128)(2,1)S(1)} all-to-all(bf16[2,1024,1,384]{3,0,2,1:T(2,128)(2,1)S(1)} %copy.338), channel_id=1, replica_groups=mesh['dp'=32,'seq'=4] {'seq'}, dimensions={1} | all-to-all | bytes 3145728 | tf_op jit(solution)/shard_map/all_to_all | solution.py:229
  261.3 11.0 %fusion.166 = (f32[2,3072]{1,0:T(2,128)}, bf16[2,256,3072]{2,1,0:T(8,128)(2,1)}, bf16[2,256,3072]{2,1,0:T(8,128)(2,1)}) fusion(bf16[2,256,3072]{2,1,0:T(8,128)(2,1)} %param.31, f32[2,3072]{1,0:T(2,128)S(1)} %copy-done.29, bf16[2,256,1536]{2,1,0:T(8,128)(2,1)} %reshape.316, bf16[1536,3072]{1,0:T(8,128)(2,1)} %param.32), kind=kOutput, calls=%fused_computation.198 | convolution fusion | flops 4842842112 | bytes 20496384 | tf_op jit(solution)/shard_map/crh,hd->crd/dot_general | solution.py:232
  274.6 2.3 copy.351
  279.3 76.6 %all-gather.2.cloned.1.call-done = bf16[2,1024,3072]{2,1,0:T(8,128)(2,1)} async-done(((bf16[2,256,3072]{2,1,0:T(8,128)(2,1)}), bf16[2,1024,3072]{2,1,0:T(8,128)(2,1)}) %all-gather.2.cloned.1.call-update) | async-done | bytes 12582928 | tf_op jit(solution)/shard_map/all_gather | solution.py:238
  355.8 13.5 %fusion.171 = bf16[2,1024,384]{1,2,0:T(8,128)(2,1)S(1)} fusion(bf16[2,1024,3072]{2,1,0:T(8,128)(2,1)} %all-gather.2.cloned.1.call-done, bf16[1536,3072]{1,0:T(8,128)(2,1)} %param.32, s32[]{:T(128)S(6)} %select_n.154), kind=kOutput, calls=%fused_computation.213 | convolution fusion | flops 4832624640 | bytes 16515076 | tf_op jit(solution)/shard_map/cnd,hd->cnh/dot_general | solution.py:240
  374.0 36.1 %while.239 = (s32[]{:T(128)}, f32[1024,3,128]{0,2,1:T(8,128)}, f32[1024,3,128]{2,0,1:T(8,128)S(1)}, f32[1024,3,128]{2,0,1:T(8,128)}, s32[]{:T(128)}, /*index=5*/...) while((s32[]{:T(128)}, f32[1024,3,128]{0,2,1:T(8,128)}, ...), condition=%wide.region_27.29_spmd, body=%wide.region_24.28_spmd.sunk | while | flops 1015355392 | bytes 44485396 | solution.py:179
  378.0 13.3 %while.245 = (s32[]{:T(128)}, f32[512,3,128]{0,2,1:T(8,128)S(1)}, f32[1024,3,128]{2,0,1:T(8,128)S(1)}, f32[1024,3,128]{2,0,1:T(8,128)}, s32[]{:T(128)}, /*index=...) while((s32[]{:T(128)}, f32[512,3,128]{0,2,1:T(8,128)S(1)}, ...), condition=%wide.region_26.27_spmd.clone.clone, body=%wide.region_25.26_spmd.clone.clone.sunk | while | flops 1015355392 | bytes 39741808 | solution.py:174
  395.9 13.2 %while.245 = (s32[]{:T(128)}, f32[512,3,128]{0,2,1:T(8,128)S(1)}, f32[1024,3,128]{2,0,1:T(8,128)S(1)}, f32[1024,3,128]{2,0,1:T(8,128)}, s32[]{:T(128)}, /*index=...) while((s32[]{:T(128)}, f32[512,3,128]{0,2,1:T(8,128)S(1)}, ...), condition=%wide.region_26.27_spmd.clone.clone, body=%wide.region_25.26_spmd.clone.clone.sunk | while | flops 1015355392 | bytes 39741808 | solution.py:174
  410.1 2.6 copy.361
  414.3 2.6 multiply_convert_fusion.1
  416.9 2.4 multiply_convert_fusion.2
  422.9 11.4 %while.237 = (s32[]{:T(128)}, f32[1024,3,128]{0,2,1:T(8,128)}, f32[1024,3,128]{2,0,1:T(8,128)S(1)}, f32[1024,3,128]{2,0,1:T(8,128)}, s32[]{:T(128)}, /*index=5*/...) while((s32[]{:T(128)}, f32[1024,3,128]{0,2,1:T(8,128)}, ...), condition=%wide.region_23.25_spmd, body=%wide.region_20.24_spmd.sunk | while | flops 1015355392 | bytes 44485404 | solution.py:179
  426.7 6.7 while.244
  434.3 2.6 copy.353
  442.0 2.6 maximum_bitcast_fusion
  444.6 12.6 %copy.362 = bf16[2,1024,3,1,384]{4,0,3,2,1:T(2,128)(2,1)} copy(bf16[2,1024,3,1,384]{1,4,2,0,3:T(8,128)(2,1)} %maximum_bitcast_fusion) | data formatting | bytes 9437184 | tf_op jit(solution)/shard_map/reshape | solution.py:264
  457.3 5.5 all-to-all-start.6
  462.8 11.1 %convolution_bitcast_fusion.4 = f32[384,3072]{0,1:T(8,128)} fusion(bf16[2,1024,3072]{2,1,0:T(8,128)(2,1)} %all-gather.2.cloned.1.call-done, bf16[1,1024,384]{2,1,0:T(8,128)(2,1)S(1)} %copy-done.22, bf16[1,1024,384]{2,1,0:T(8,128)(2,1)S(1)} %copy-done.23), kind=kOutput, calls=%fused_computation.204 | convolution fusion | flops 4832624640 | bytes 18874368 | tf_op jit(solution)/shard_map/cnh,cnd->hd/dot_general | solution.py:239
  473.9 96.9 %all-to-all-done.6 = bf16[2,1024,3,1,384]{4,0,3,2,1:T(2,128)(2,1)} async-done(((bf16[2,1024,3,1,384]{4,0,3,2,1:T(2,128)(2,1)}), bf16[2,1024,3,1,384]{4,0,3,2,1:T(2,128)(2,1)}, u32[]{:S(2)}, u32[]{:S(2)}) %all-to-all-start.6) | async-done | bytes 4718624 | tf_op jit(solution)/shard_map/all_to_all | solution.py:265
  570.8 3.0 copy.363
  577.5 2.4 reshape_squeeze.39
  579.9 14.0 %all-to-all-start.7 = ((bf16[32,8,4608]{2,1,0:T(8,128)(2,1)}), bf16[32,8,4608]{2,1,0:T(8,128)(2,1)S(1)}, u32[]{:S(2)}, u32[]{:S(2)}) async-start(bf16[32,8,4608]{2,1,0:T(8,128)(2,1)} %reshape_squeeze.39), calls=%async_computation.8 | async-start | bytes 4718592 | tf_op jit(solution)/shard_map/all_to_all | solution.py:39
  593.9 28.4 %all-to-all-done.7 = bf16[32,8,4608]{2,1,0:T(8,128)(2,1)S(1)} async-done(((bf16[32,8,4608]{2,1,0:T(8,128)(2,1)}), bf16[32,8,4608]{2,1,0:T(8,128)(2,1)S(1)}, u32[]{:S(2)}, u32[]{:S(2)}) %all-to-all-start.7) | async-done | bytes 2359328 | tf_op jit(solution)/shard_map/all_to_all | solution.py:39
  622.9 9.2 %all-to-all-start.4 = ((f32[4,2,3072]{2,1,0:T(2,128)}), f32[4,2,3072]{2,1,0:T(2,128)S(1)}, u32[]{:S(2)}, u32[]{:S(2)}) async-start(f32[4,2,3072]{2,1,0:T(2,128)} %broadcast_in_dim.133), calls=%async_computation.4 | async-start | bytes 196608 | tf_op jit(solution)/shard_map/all_to_all | solution.py:14
  632.1 2.1 gather_fusion.1
  634.3 3.4 broadcast_select_fusion
  638.2 6.1 all-to-all-start.8
  645.0 4.3 copy.364
  649.3 25.0 %all-to-all-done.8 = bf16[32,8,4608]{2,1,0:T(8,128)(2,1)S(1)} async-done(((bf16[32,8,4608]{2,1,0:T(8,128)(2,1)}), bf16[32,8,4608]{2,1,0:T(8,128)(2,1)S(1)}, u32[]{:S(2)}, u32[]{:S(2)}) %all-to-all-start.8) | async-done | bytes 2359328 | tf_op jit(solution)/shard_map/all_to_all | solution.py:41
  674.3 2.5 copy.366
  676.8 13.5 %all-to-all-start.5 = ((f32[384,4,24]{0,2,1:T(8,128)}), f32[384,4,24]{0,2,1:T(8,128)S(1)}, u32[]{:S(2)}, u32[]{:S(2)}) async-start(f32[384,4,24]{0,2,1:T(8,128)} %bitcast.308), calls=%async_computation.6 | async-start | bytes 294912 | tf_op jit(solution)/shard_map/all_to_all | solution.py:245
  690.3 5.0 pad_maximum_fusion.1
  695.3 6.6 copy.367
  (260 shorter events, 112.5 us)
Async XLA Ops:
  12.0 9.4 %copy-start.30 = (s32[32]{0:T(128)S(1)}, s32[32]{0:T(128)}, u32[]{:S(2)}) copy-start(s32[32]{0:T(128)} %param.35) | copy-start | bytes 388
  12.0 40.1 %all-to-all-start = ((bf16[32,8,4608]{2,1,0:T(8,128)(2,1)}), bf16[32,8,4608]{2,1,0:T(8,128)(2,1)S(1)}, u32[]{:S(2)}, u32[]{:S(2)}) async-start(bf16[32,8,4608]{2,1,0:T(8,128)(2,1)} %get-tuple-element.2898), calls=%async_computation | async-start | bytes 4718592 | tf_op jit(solution)/shard_map/all_to_all | solution.py:30
  57.6 34.4 %all-to-all-start.1 = ((bf16[32,8,4608]{2,1,0:T(8,128)(2,1)}), bf16[32,8,4608]{2,1,0:T(8,128)(2,1)S(1)}, u32[]{:S(2)}, u32[]{:S(2)}) async-start(bf16[32,8,4608]{2,1,0:T(8,128)(2,1)} %broadcast_select_fusion.1), calls=%async_computation.1 | async-start | bytes 4718592 | tf_op jit(solution)/shard_map/all_to_all | solution.py:32
  94.1 5.5 copy-start.10
  104.3 9.5 %copy-start.27 = (s32[64]{0:T(128)S(1)}, s32[64]{0:T(128)}, u32[]{:S(2)}) copy-start(s32[64]{0:T(128)} %param.34) | copy-start | bytes 772
  104.3 9.5 %copy-start.28 = (s32[64]{0:T(128)S(1)}, s32[64]{0:T(128)}, u32[]{:S(2)}) copy-start(s32[64]{0:T(128)} %param.33) | copy-start | bytes 772
  104.3 62.6 %all-to-all-start.2 = ((bf16[2,256,3,4,384]{1,4,2,0,3:T(8,128)(2,1)}), bf16[2,256,3,4,384]{1,4,2,0,3:T(8,128)(2,1)}, u32[]{:S(2)}, u32[]{:S(2)}) async-start(bf16[2,256,3,4,384]{1,4,2,0,3:T(8,128)(2,1)} %copy.326), calls=%async_computation.2 | async-start | bytes 9437184 | tf_op jit(solution)/shard_map/all_to_all | solution.py:49
  112.5 243.3 %all-gather.2.cloned.1.call-start = ((), (), s32[]{:S(2)}) async-start(), calls=%async_computation.10 | async-start | bytes 15728640 | tf_op jit(solution)/shard_map/all_gather | solution.py:238
  207.0 6.1 copy-start.6
  207.0 4.9 copy-start.16
  227.1 7.3 %copy-start = (bf16[1024,3,128]{2,0,1:T(8,128)(2,1)}, bf16[1024,3,128]{2,0,1:T(8,128)(2,1)S(1)}, u32[]{:S(2)}) copy-start(bf16[1024,3,128]{2,0,1:T(8,128)(2,1)S(1)} %get-tuple-element.4344) | copy-start | bytes 2359300
  259.8 1.5 copy-start.29
  272.3 1.1 copy-start.17
  272.3 4.6 copy-start.7
  273.4 4.7 copy-start.4
  370.4 2.3 copy-start.3
  378.0 1.4 copy-start.8
  378.0 1.4 copy-start.25
  381.0 1.4 copy-start.11
  383.4 1.1 copy-start.12
  384.6 1.4 copy-start.8
  384.6 1.4 copy-start.25
  387.6 1.4 copy-start.11
  390.1 1.1 copy-start.12
  395.9 1.4 copy-start.8
  396.0 1.4 copy-start.25
  399.0 1.4 copy-start.11
  401.4 1.1 copy-start.12
  402.6 1.4 copy-start.8
  402.6 1.4 copy-start.25
  405.6 1.4 copy-start.11
  408.0 1.1 copy-start.12
  414.3 5.0 copy-start.2
  414.3 5.0 copy-start.5
  420.2 2.7 copy-start.1
  426.7 1.4 copy-start.9
  426.7 1.4 copy-start.24
  429.8 1.4 copy-start.14
  432.3 1.1 copy-start.15
  436.9 3.3 copy-start.13
  438.6 1.9 copy-start.18
  438.6 1.9 copy-start.19
  438.6 2.1 copy-start.20
  440.6 1.1 copy-start.21
  457.3 5.5 copy-start.22
  457.3 5.5 copy-start.23
  457.3 113.5 %all-to-all-start.6 = ((bf16[2,1024,3,1,384]{4,0,3,2,1:T(2,128)(2,1)}), bf16[2,1024,3,1,384]{4,0,3,2,1:T(2,128)(2,1)}, u32[]{:S(2)}, u32[]{:S(2)}) async-start(bf16[2,1024,3,1,384]{4,0,3,2,1:T(2,128)(2,1)} %copy.362), calls=%async_computation.7 | async-start | bytes 9437184 | tf_op jit(solution)/shard_map/all_to_all | solution.py:265
  462.8 214.0 %reduce-scatter.2.cloned.1.call-start = ((), (), s32[]{:S(2)}) async-start(), calls=%async_computation.11 | async-start | bytes 4866048 | tf_op jit(solution)/shard_map/reduce_scatter | solution.py:244
  579.9 14.0 %copy-start.31 = (s32[32]{0:T(128)S(1)}, s32[32]{0:T(128)}, u32[]{:S(2)}) copy-start(s32[32]{0:T(128)} %param.35) | copy-start | bytes 388
  579.9 42.4 %copy-start.26 = (f32[2,3072]{1,0:T(2,128)S(1)}, f32[2,3072]{1,0:T(2,128)}, u32[]{:S(2)}) copy-start(f32[2,3072]{1,0:T(2,128)} %get-tuple-element.2887) | copy-start | bytes 73732
  579.9 42.4 %all-to-all-start.7 = ((bf16[32,8,4608]{2,1,0:T(8,128)(2,1)}), bf16[32,8,4608]{2,1,0:T(8,128)(2,1)S(1)}, u32[]{:S(2)}, u32[]{:S(2)}) async-start(bf16[32,8,4608]{2,1,0:T(8,128)(2,1)} %reshape_squeeze.39), calls=%async_computation.8 | async-start | bytes 4718592 | tf_op jit(solution)/shard_map/all_to_all | solution.py:39
  622.9 15.3 %all-to-all-start.4 = ((f32[4,2,3072]{2,1,0:T(2,128)}), f32[4,2,3072]{2,1,0:T(2,128)S(1)}, u32[]{:S(2)}, u32[]{:S(2)}) async-start(f32[4,2,3072]{2,1,0:T(2,128)} %broadcast_in_dim.133), calls=%async_computation.4 | async-start | bytes 196608 | tf_op jit(solution)/shard_map/all_to_all | solution.py:14
  638.2 36.1 %all-to-all-start.8 = ((bf16[32,8,4608]{2,1,0:T(8,128)(2,1)}), bf16[32,8,4608]{2,1,0:T(8,128)(2,1)S(1)}, u32[]{:S(2)}, u32[]{:S(2)}) async-start(bf16[32,8,4608]{2,1,0:T(8,128)(2,1)} %broadcast_select_fusion), calls=%async_computation.9 | async-start | bytes 4718592 | tf_op jit(solution)/shard_map/all_to_all | solution.py:41
  676.8 25.1 %all-to-all-start.5 = ((f32[384,4,24]{0,2,1:T(8,128)}), f32[384,4,24]{0,2,1:T(8,128)S(1)}, u32[]{:S(2)}, u32[]{:S(2)}) async-start(f32[384,4,24]{0,2,1:T(8,128)} %bitcast.308), calls=%async_computation.6 | async-start | bytes 294912 | tf_op jit(solution)/shard_map/all_to_all | solution.py:245
Sparse Core Ops, SparseCore 0:
  272.5 83.3 all-gather.1
  474.1 177.7 reduce-scatter.1
where the time goes:
time: 720 us; the launch traced here: 710 us
  waiting for transfers between devices  334 us (46%)
  local copies, waits for them, and re-layouts  144 us (20%)
  matrix products  70.4 us (10%)
  starting transfers between devices  70.2 us (10%)
  other arithmetic  47.2 us (7%)
  blocking collectives  24 us (3%)
  between operations  17.9 us (2%)
    all_to_all x1, waiting for transfers between devices, body(): lax.all_to_all(grad_heads, 'seq', split_axis=1, concat_axis=3, tiled=True)  96.9 us
    all_gather x1, waiting for transfers between devices, body(): portion = lax.all_gather(scaled, 'seq', axis=1, tiled=True)  76.6 us
    all_to_all x1, waiting for transfers between devices, to_heads(): lax.all_to_all(parted, 'seq', split_axis=3, concat_axis=1, tiled=True)  49.8 us
    all_to_all x1, waiting for transfers between devices, move_in(): lax.all_to_all(portions, 'dp', split_axis=0, concat_axis=0, tiled=True)  30.6 us
    all_to_all x1, waiting for transfers between devices, move_out(): lax.all_to_all(portions, 'dp', split_axis=0, concat_axis=0, tiled=True)  28.4 us
    all_to_all x1, waiting for transfers between devices, move_in(): lax.all_to_all(arranged, 'dp', split_axis=0, concat_axis=0, tiled=True)  25.9 us
    all_to_all x1, waiting for transfers between devices, move_out(): lax.all_to_all(arranged, 'dp', split_axis=0, concat_axis=0, tiled=True)  25 us
    all_to_all x1, blocking collectives, body(): lax.all_to_all(attn_heads, 'seq', split_axis=1, concat_axis=2, tiled=True)  24 us
  transfers between devices with their start and end apart: 10, of which 8 were waited for; matrix products, arithmetic and copies ran while one was open for 8% of the time, Pallas kernels for 0%

commit v1 on v0

--- a/solution.py
+++ b/solution.py
@@ -235,7 +235,9 @@
     scaled = (cotangent.astype(jnp.float32) * gate[:, None, :]).astype(jnp.bfloat16)
     weight_rows = lax.dynamic_slice_in_dim(out_weight, seq_index * local_width, local_width, 0)
     flat_heads = attn_heads.reshape(2, seq_len, local_width)
-    portion = lax.all_gather(scaled, "seq", axis=1, tiled=True)
+    portion = jnp.concatenate(
+        lax.all_to_all(jnp.stack([scaled] * lax.axis_size("seq")), "seq", 0, 0), axis=1
+    )
     weight_part = jnp.einsum("cnh,cnd->hd", flat_heads, portion, preferred_element_type=jnp.float32)
     grad_rows = jnp.einsum(
         "cnd,hd->cnh", portion, weight_rows, preferred_element_type=jnp.float32

time: 720 us -> 796 us (1.11)
  waiting for transfers between devices: 334 us -> 394 us
  local copies, waits for them, and re-layouts: 144 us -> 162 us
    all_to_all x0 -> x1, waiting for transfers between devices: none -> 133 us  [body(): lax.all_to_all(jnp.stack([scaled] * lax.axis_size('seq')), 'seq', 0, 0)]
    all_gather x1 -> x0, waiting for transfers between devices: 76.6 us -> none  [body(): portion = lax.all_gather(scaled, 'seq', axis=1, tiled=True)]
  transfers between devices with their start and end apart: 10 -> 10, of which waited for: 8 -> 8; matrix products, arithmetic and copies ran while one was open for 8% -> 7% of each run, Pallas kernels for 0% -> 0%
where the time goes in v1:
time: 796 us; the launch traced here: 785 us
  waiting for transfers between devices  394 us (49%)
  local copies, waits for them, and re-layouts  162 us (20%)
  starting transfers between devices  72.1 us (9%)
  matrix products  65.2 us (8%)
  other arithmetic  46.1 us (6%)
  blocking collectives  25.1 us (3%)
  between operations  18.2 us (2%)
    all_to_all x1, waiting for transfers between devices, body(): lax.all_to_all(jnp.stack([scaled] * lax.axis_size('seq')), 'seq', 0, 0)  133 us
    all_to_all x1, waiting for transfers between devices, body(): lax.all_to_all(grad_heads, 'seq', split_axis=1, concat_axis=3, tiled=True)  100 us
    all_to_all x1, waiting for transfers between devices, to_heads(): lax.all_to_all(parted, 'seq', split_axis=3, concat_axis=1, tiled=True)  49.8 us
    all_to_all x1, waiting for transfers between devices, move_in(): lax.all_to_all(portions, 'dp', split_axis=0, concat_axis=0, tiled=True)  30.6 us
    all_to_all x1, waiting for transfers between devices, move_out(): lax.all_to_all(portions, 'dp', split_axis=0, concat_axis=0, tiled=True)  27.7 us
    all_to_all x1, waiting for transfers between devices, move_out(): lax.all_to_all(arranged, 'dp', split_axis=0, concat_axis=0, tiled=True)  25.9 us
    all_to_all x1, waiting for transfers between devices, move_in(): lax.all_to_all(arranged, 'dp', split_axis=0, concat_axis=0, tiled=True)  25.9 us
    all_to_all x1, blocking collectives, body(): lax.all_to_all(attn_heads, 'seq', split_axis=1, concat_axis=2, tiled=True)  25.1 us
  transfers between devices with their start and end apart: 10, of which 8 were waited for; matrix products, arithmetic and copies ran while one was open for 7% of the time, Pallas kernels for 0%

profile of v1, /device:TPU:1, one launch (start us, length us, event | category | flops | bytes accessed | tf_op | source)
XLA Modules:
  0.0 784.7 jit_solution(17254479885756078074)
XLA Ops:
  7.2 4.9 fusion.183
  12.0 9.3 %all-to-all-start = ((bf16[32,8,4608]{2,1,0:T(8,128)(2,1)}), bf16[32,8,4608]{2,1,0:T(8,128)(2,1)S(1)}, u32[]{:S(2)}, u32[]{:S(2)}) async-start(bf16[32,8,4608]{2,1,0:T(8,128)(2,1)} %get-tuple-element.2898), calls=%async_computation | async-start | bytes 4718592 | tf_op jit(solution)/shard_map/all_to_all | solution.py:30
  21.5 30.6 %all-to-all-done = bf16[32,8,4608]{2,1,0:T(8,128)(2,1)S(1)} async-done(((bf16[32,8,4608]{2,1,0:T(8,128)(2,1)}), bf16[32,8,4608]{2,1,0:T(8,128)(2,1)S(1)}, u32[]{:S(2)}, u32[]{:S(2)}) %all-to-all-start) | async-done | bytes 2359328 | tf_op jit(solution)/shard_map/all_to_all | solution.py:30
  54.3 3.3 broadcast_select_fusion.1
  57.6 4.2 all-to-all-start.1
  61.9 4.3 copy.404
  66.1 25.9 %all-to-all-done.1 = bf16[32,8,4608]{2,1,0:T(8,128)(2,1)S(1)} async-done(((bf16[32,8,4608]{2,1,0:T(8,128)(2,1)}), bf16[32,8,4608]{2,1,0:T(8,128)(2,1)S(1)}, u32[]{:S(2)}, u32[]{:S(2)}) %all-to-all-start.1) | async-done | bytes 2359328 | tf_op jit(solution)/shard_map/all_to_all | solution.py:32
  94.1 5.5 copy.335
  101.8 2.5 copy.336
  104.3 8.3 %all-to-all-start.2 = ((bf16[2,256,3,4,384]{1,4,2,0,3:T(8,128)(2,1)}), bf16[2,256,3,4,384]{1,4,2,0,3:T(8,128)(2,1)}, u32[]{:S(2)}, u32[]{:S(2)}) async-start(bf16[2,256,3,4,384]{1,4,2,0,3:T(8,128)(2,1)} %copy.336), calls=%async_computation.2 | async-start | bytes 9437184 | tf_op jit(solution)/shard_map/all_to_all | solution.py:49
  117.1 49.8 %all-to-all-done.2 = bf16[2,256,3,4,384]{1,4,2,0,3:T(8,128)(2,1)} async-done(((bf16[2,256,3,4,384]{1,4,2,0,3:T(8,128)(2,1)}), bf16[2,256,3,4,384]{1,4,2,0,3:T(8,128)(2,1)}, u32[]{:S(2)}, u32[]{:S(2)}) %all-to-all-start.2) | async-done | bytes 4718624 | tf_op jit(solution)/shard_map/all_to_all | solution.py:49
  166.9 6.6 copy.337
  173.5 3.9 fusion.182
  181.5 26.0 %while.235 = (s32[]{:T(128)}, bf16[1024,3,128]{0,2,1:T(8,128)(2,1)S(1)}, f32[3,1024]{1,0:T(4,128)}, s32[]{:T(128)}, bf16[1024,3,128]{2,0,1:T(8,128)(2,1)}, /*ind...) while((s32[]{:T(128)}, ...), condition=%wide.region_16.18_spmd, body=%wide.region_9.17_spmd.sunk | while | flops 613564928 | bytes 14026645 | solution.py:118
  182.6 4.7 while.242
  187.9 6.5 while.243
  188.8 2.4 fusion.293
  192.0 2.4 fusion.293
  195.6 4.7 while.242
  201.0 6.5 while.243
  201.8 2.4 fusion.293
  205.1 2.4 fusion.293
  207.5 2.9 copy.338
  210.4 2.3 copy.341
  218.4 8.0 %while.232 = (s32[]{:T(128)}, bf16[1024,3,128]{0,2,1:T(8,128)(2,1)S(1)}, f32[3,1024]{1,0:T(4,128)}, s32[]{:T(128)}, bf16[1024,3,128]{2,0,1:T(8,128)(2,1)}, /*ind...) while((s32[]{:T(128)}, ...), condition=%wide.region_8.10_spmd, body=%wide.region_1.9_spmd.sunk | while | flops 613564928 | bytes 14026645 | solution.py:118
  220.0 2.4 while.240
  223.1 3.3 while.241
  224.0 2.4 fusion.301
  226.4 3.0 pad_maximum_fusion.2
  229.4 4.9 copy.348
  234.4 25.1 %all_to_all.94 = bf16[2,1024,1,384]{3,0,2,1:T(2,128)(2,1)S(1)} all-to-all(bf16[2,1024,1,384]{3,0,2,1:T(2,128)(2,1)} %copy.348), channel_id=1, replica_groups=mesh['dp'=32,'seq'=4] {'seq'}, dimensions={1} | all-to-all | bytes 3145728 | tf_op jit(solution)/shard_map/all_to_all | solution.py:229
  262.4 11.0 %fusion.166 = (f32[2,3072]{1,0:T(2,128)}, bf16[2,256,3072]{2,1,0:T(8,128)(2,1)}, bf16[2,256,3072]{2,1,0:T(8,128)(2,1)}) fusion(bf16[2,256,3072]{2,1,0:T(8,128)(2,1)} %param.31, f32[2,3072]{1,0:T(2,128)S(1)} %copy-done.33, bf16[2,256,1536]{2,1,0:T(8,128)(2,1)} %reshape.324, bf16[1536,3072]{1,0:T(8,128)(2,1)} %param.32), kind=kOutput, calls=%fused_computation.198 | convolution fusion | flops 4842842112 | bytes 20496384 | tf_op jit(solution)/shard_map/crh,hd->crd/dot_general | solution.py:232
  273.4 4.6 copy.354
  278.0 7.3 stack.56
  285.3 7.6 all-to-all-start.5
  298.8 132.8 %all-to-all-done.5 = bf16[4,2,256,3072]{2,3,1,0:T(8,128)(2,1)} async-done(((bf16[4,2,256,3072]{2,3,1,0:T(8,128)(2,1)}), bf16[4,2,256,3072]{2,3,1,0:T(8,128)(2,1)}, u32[]{:S(2)}, u32[]{:S(2)}) %all-to-all-start.5) | async-done | bytes 12582944 | tf_op jit(solution)/shard_map/all_to_all | solution.py:239
  431.5 6.6 copy.407
  438.1 7.7 fusion.171
  450.5 36.2 %while.239 = (s32[]{:T(128)}, f32[1024,3,128]{0,2,1:T(8,128)}, f32[1024,3,128]{2,0,1:T(8,128)S(1)}, f32[1024,3,128]{2,0,1:T(8,128)}, s32[]{:T(128)}, /*index=5*/...) while((s32[]{:T(128)}, f32[1024,3,128]{0,2,1:T(8,128)}, ...), condition=%wide.region_27.29_spmd, body=%wide.region_24.28_spmd.sunk | while | flops 1015355392 | bytes 44485404 | solution.py:179
  454.3 13.4 %while.245 = (s32[]{:T(128)}, f32[512,3,128]{0,2,1:T(8,128)S(1)}, f32[1024,3,128]{2,0,1:T(8,128)S(1)}, f32[1024,3,128]{2,0,1:T(8,128)}, s32[]{:T(128)}, /*index=...) while((s32[]{:T(128)}, f32[512,3,128]{0,2,1:T(8,128)S(1)}, ...), condition=%wide.region_26.27_spmd.clone.clone, body=%wide.region_25.26_spmd.clone.clone.sunk | while | flops 1015355392 | bytes 39741808 | solution.py:174
  472.4 13.4 %while.245 = (s32[]{:T(128)}, f32[512,3,128]{0,2,1:T(8,128)S(1)}, f32[1024,3,128]{2,0,1:T(8,128)S(1)}, f32[1024,3,128]{2,0,1:T(8,128)}, s32[]{:T(128)}, /*index=...) while((s32[]{:T(128)}, f32[512,3,128]{0,2,1:T(8,128)S(1)}, ...), condition=%wide.region_26.27_spmd.clone.clone, body=%wide.region_25.26_spmd.clone.clone.sunk | while | flops 1015355392 | bytes 39741808 | solution.py:174
  486.7 2.6 copy.373
  490.9 2.6 multiply_convert_fusion.1
  498.2 11.7 %while.237 = (s32[]{:T(128)}, f32[1024,3,128]{0,2,1:T(8,128)}, f32[1024,3,128]{2,0,1:T(8,128)S(1)}, f32[1024,3,128]{2,0,1:T(8,128)}, s32[]{:T(128)}, /*index=5*/...) while((s32[]{:T(128)}, f32[1024,3,128]{0,2,1:T(8,128)}, ...), condition=%wide.region_23.25_spmd, body=%wide.region_20.24_spmd.sunk | while | flops 1015355392 | bytes 44485404 | solution.py:179
  502.2 6.8 while.244
  509.9 2.6 copy.365
  517.5 2.6 maximum_bitcast_fusion
  520.1 12.6 %copy.374 = bf16[2,1024,3,1,384]{4,0,3,2,1:T(2,128)(2,1)} copy(bf16[2,1024,3,1,384]{1,4,2,0,3:T(8,128)(2,1)} %maximum_bitcast_fusion) | data formatting | bytes 9437184 | tf_op jit(solution)/shard_map/reshape | solution.py:266
  532.8 6.0 all-to-all-start.7
  539.0 11.9 %convolution_bitcast_fusion.4 = f32[384,3072]{0,1:T(8,128)} fusion(bf16[2,1024,3072]{1,2,0:T(8,128)(2,1)} %bitcast.291, bf16[1,1024,384]{2,1,0:T(8,128)(2,1)S(1)} %copy-done.26, bf16[1,1024,384]{2,1,0:T(8,128)(2,1)S(1)} %copy-done.27), kind=kOutput, calls=%fused_computation.204 | convolution fusion | flops 4832624640 | bytes 18874368 | tf_op jit(solution)/shard_map/cnh,cnd->hd/dot_general | solution.py:241
  550.9 100.3 %all-to-all-done.7 = bf16[2,1024,3,1,384]{4,0,3,2,1:T(2,128)(2,1)} async-done(((bf16[2,1024,3,1,384]{4,0,3,2,1:T(2,128)(2,1)}), bf16[2,1024,3,1,384]{4,0,3,2,1:T(2,128)(2,1)}, u32[]{:S(2)}, u32[]{:S(2)}) %all-to-all-start.7) | async-done | bytes 4718624 | tf_op jit(solution)/shard_map/all_to_all | solution.py:267
  651.2 3.0 copy.375
  657.9 2.4 reshape_squeeze.39
  660.3 8.9 %all-to-all-start.8 = ((bf16[32,8,4608]{2,1,0:T(8,128)(2,1)}), bf16[32,8,4608]{2,1,0:T(8,128)(2,1)S(1)}, u32[]{:S(2)}, u32[]{:S(2)}) async-start(bf16[32,8,4608]{2,1,0:T(8,128)(2,1)} %reshape_squeeze.39), calls=%async_computation.9 | async-start | bytes 4718592 | tf_op jit(solution)/shard_map/all_to_all | solution.py:39
  669.2 27.7 %all-to-all-done.8 = bf16[32,8,4608]{2,1,0:T(8,128)(2,1)S(1)} async-done(((bf16[32,8,4608]{2,1,0:T(8,128)(2,1)}), bf16[32,8,4608]{2,1,0:T(8,128)(2,1)S(1)}, u32[]{:S(2)}, u32[]{:S(2)}) %all-to-all-start.8) | async-done | bytes 2359328 | tf_op jit(solution)/shard_map/all_to_all | solution.py:39
  697.6 9.2 %all-to-all-start.4 = ((f32[4,2,3072]{2,1,0:T(2,128)}), f32[4,2,3072]{2,1,0:T(2,128)S(1)}, u32[]{:S(2)}, u32[]{:S(2)}) async-start(f32[4,2,3072]{2,1,0:T(2,128)} %broadcast_in_dim.133), calls=%async_computation.4 | async-start | bytes 196608 | tf_op jit(solution)/shard_map/all_to_all | solution.py:14
  708.9 3.4 broadcast_select_fusion
  713.4 6.6 all-to-all-start.9
  720.6 4.3 copy.376
  724.9 25.9 %all-to-all-done.9 = bf16[32,8,4608]{2,1,0:T(8,128)(2,1)S(1)} async-done(((bf16[32,8,4608]{2,1,0:T(8,128)(2,1)}), bf16[32,8,4608]{2,1,0:T(8,128)(2,1)S(1)}, u32[]{:S(2)}, u32[]{:S(2)}) %all-to-all-start.9) | async-done | bytes 2359328 | tf_op jit(solution)/shard_map/all_to_all | solution.py:41
  750.9 2.5 copy.378
  753.4 11.8 %all-to-all-start.6 = ((f32[384,4,24]{0,2,1:T(8,128)}), f32[384,4,24]{0,2,1:T(8,128)S(1)}, u32[]{:S(2)}, u32[]{:S(2)}) async-start(f32[384,4,24]{0,2,1:T(8,128)} %bitcast.313), calls=%async_computation.7 | async-start | bytes 294912 | tf_op jit(solution)/shard_map/all_to_all | solution.py:247
  765.2 5.0 pad_maximum_fusion.1
  770.1 6.6 copy.379
  (270 shorter events, 119.4 us)
Async XLA Ops:
  12.0 9.4 %copy-start.34 = (s32[32]{0:T(128)S(1)}, s32[32]{0:T(128)}, u32[]{:S(2)}) copy-start(s32[32]{0:T(128)} %param.35) | copy-start | bytes 388
  12.0 40.1 %all-to-all-start = ((bf16[32,8,4608]{2,1,0:T(8,128)(2,1)}), bf16[32,8,4608]{2,1,0:T(8,128)(2,1)S(1)}, u32[]{:S(2)}, u32[]{:S(2)}) async-start(bf16[32,8,4608]{2,1,0:T(8,128)(2,1)} %get-tuple-element.2898), calls=%async_computation | async-start | bytes 4718592 | tf_op jit(solution)/shard_map/all_to_all | solution.py:30
  57.6 34.4 %all-to-all-start.1 = ((bf16[32,8,4608]{2,1,0:T(8,128)(2,1)}), bf16[32,8,4608]{2,1,0:T(8,128)(2,1)S(1)}, u32[]{:S(2)}, u32[]{:S(2)}) async-start(bf16[32,8,4608]{2,1,0:T(8,128)(2,1)} %broadcast_select_fusion.1), calls=%async_computation.1 | async-start | bytes 4718592 | tf_op jit(solution)/shard_map/all_to_all | solution.py:32
  94.1 5.5 copy-start.13
  104.3 9.5 %copy-start.31 = (s32[64]{0:T(128)S(1)}, s32[64]{0:T(128)}, u32[]{:S(2)}) copy-start(s32[64]{0:T(128)} %param.34) | copy-start | bytes 772
  104.3 9.5 %copy-start.32 = (s32[64]{0:T(128)S(1)}, s32[64]{0:T(128)}, u32[]{:S(2)}) copy-start(s32[64]{0:T(128)} %param.33) | copy-start | bytes 772
  104.3 62.6 %all-to-all-start.2 = ((bf16[2,256,3,4,384]{1,4,2,0,3:T(8,128)(2,1)}), bf16[2,256,3,4,384]{1,4,2,0,3:T(8,128)(2,1)}, u32[]{:S(2)}, u32[]{:S(2)}) async-start(bf16[2,256,3,4,384]{1,4,2,0,3:T(8,128)(2,1)} %copy.336), calls=%async_computation.2 | async-start | bytes 9437184 | tf_op jit(solution)/shard_map/all_to_all | solution.py:49
  207.5 7.5 copy-start
  207.5 7.5 copy-start.9
  210.4 6.2 copy-start.20
  226.4 7.9 %copy-start.2 = (bf16[1024,3,128]{2,0,1:T(8,128)(2,1)}, bf16[1024,3,128]{2,0,1:T(8,128)(2,1)S(1)}, u32[]{:S(2)}) copy-start(bf16[1024,3,128]{2,0,1:T(8,128)(2,1)S(1)} %get-tuple-element.4366) | copy-start | bytes 2359300
  226.4 71.2 %copy-start.7 = (bf16[1024,3,128]{0,2,1:T(8,128)(2,1)}, bf16[1024,3,128]{0,2,1:T(8,128)(2,1)S(1)}, u32[]{:S(2)}) copy-start(bf16[1024,3,128]{0,2,1:T(8,128)(2,1)S(1)} %get-tuple-element.1855) | copy-start | bytes 2359300
  260.8 1.5 copy-start.33
  285.3 7.6 copy-start.21
  285.3 146.2 %all-to-all-start.5 = ((bf16[4,2,256,3072]{2,3,1,0:T(8,128)(2,1)}), bf16[4,2,256,3072]{2,3,1,0:T(8,128)(2,1)}, u32[]{:S(2)}, u32[]{:S(2)}) async-start(bf16[4,2,256,3072]{2,3,1,0:T(8,128)(2,1)} %stack.56), calls=%async_computation.5 | async-start | bytes 25165824 | tf_op jit(solution)/shard_map/all_to_all | solution.py:239
  292.9 3.5 copy-start.10
  438.1 7.7 copy-start.6
  446.9 2.3 copy-start.5
  447.8 2.7 copy-start.1
  454.3 1.4 copy-start.11
  454.3 1.4 copy-start.29
  457.4 1.4 copy-start.15
  459.8 1.2 copy-start.16
  461.0 1.4 copy-start.11
  461.0 1.4 copy-start.29
  464.1 1.4 copy-start.15
  466.5 1.2 copy-start.16
  472.4 1.4 copy-start.11
  472.4 1.4 copy-start.29
  475.5 1.4 copy-start.15
  478.0 1.2 copy-start.16
  479.1 1.4 copy-start.11
  479.1 1.4 copy-start.29
  482.2 1.4 copy-start.15
  484.6 1.2 copy-start.16
  489.3 4.2 copy-start.14
  490.9 3.6 copy-start.4
  490.9 3.6 copy-start.8
  495.5 2.7 copy-start.3
  502.2 1.5 copy-start.12
  502.2 1.5 copy-start.28
  505.3 1.4 copy-start.18
  507.8 1.2 copy-start.19
  512.4 3.3 copy-start.17
  514.1 1.9 copy-start.22
  514.1 1.9 copy-start.23
  514.1 2.1 copy-start.24
  516.1 1.1 copy-start.25
  532.8 6.3 copy-start.26
  532.8 6.3 copy-start.27
  532.8 118.5 %all-to-all-start.7 = ((bf16[2,1024,3,1,384]{4,0,3,2,1:T(2,128)(2,1)}), bf16[2,1024,3,1,384]{4,0,3,2,1:T(2,128)(2,1)}, u32[]{:S(2)}, u32[]{:S(2)}) async-start(bf16[2,1024,3,1,384]{4,0,3,2,1:T(2,128)(2,1)} %copy.374), calls=%async_computation.8 | async-start | bytes 9437184 | tf_op jit(solution)/shard_map/all_to_all | solution.py:267
  538.8 214.6 %reduce-scatter.2.cloned.1.call-start = ((), (), s32[]{:S(2)}) async-start(), calls=%async_computation.11 | async-start | bytes 4866048 | tf_op jit(solution)/shard_map/reduce_scatter | solution.py:246
  660.3 8.9 %copy-start.35 = (s32[32]{0:T(128)S(1)}, s32[32]{0:T(128)}, u32[]{:S(2)}) copy-start(s32[32]{0:T(128)} %param.35) | copy-start | bytes 388
  660.3 36.6 %copy-start.30 = (f32[2,3072]{1,0:T(2,128)S(1)}, f32[2,3072]{1,0:T(2,128)}, u32[]{:S(2)}) copy-start(f32[2,3072]{1,0:T(2,128)} %get-tuple-element.2887) | copy-start | bytes 73732
  660.3 36.6 %all-to-all-start.8 = ((bf16[32,8,4608]{2,1,0:T(8,128)(2,1)}), bf16[32,8,4608]{2,1,0:T(8,128)(2,1)S(1)}, u32[]{:S(2)}, u32[]{:S(2)}) async-start(bf16[32,8,4608]{2,1,0:T(8,128)(2,1)} %reshape_squeeze.39), calls=%async_computation.9 | async-start | bytes 4718592 | tf_op jit(solution)/shard_map/all_to_all | solution.py:39
  697.6 15.8 %all-to-all-start.4 = ((f32[4,2,3072]{2,1,0:T(2,128)}), f32[4,2,3072]{2,1,0:T(2,128)S(1)}, u32[]{:S(2)}, u32[]{:S(2)}) async-start(f32[4,2,3072]{2,1,0:T(2,128)} %broadcast_in_dim.133), calls=%async_computation.4 | async-start | bytes 196608 | tf_op jit(solution)/shard_map/all_to_all | solution.py:14
  713.4 37.5 %all-to-all-start.9 = ((bf16[32,8,4608]{2,1,0:T(8,128)(2,1)}), bf16[32,8,4608]{2,1,0:T(8,128)(2,1)S(1)}, u32[]{:S(2)}, u32[]{:S(2)}) async-start(bf16[32,8,4608]{2,1,0:T(8,128)(2,1)} %broadcast_select_fusion), calls=%async_computation.10 | async-start | bytes 4718592 | tf_op jit(solution)/shard_map/all_to_all | solution.py:41
  753.4 23.4 %all-to-all-start.6 = ((f32[384,4,24]{0,2,1:T(8,128)}), f32[384,4,24]{0,2,1:T(8,128)S(1)}, u32[]{:S(2)}, u32[]{:S(2)}) async-start(f32[384,4,24]{0,2,1:T(8,128)} %bitcast.313), calls=%async_computation.7 | async-start | bytes 294912 | tf_op jit(solution)/shard_map/all_to_all | solution.py:247
Sparse Core Ops, SparseCore 0:
  551.1 172.5 reduce-scatter.1
